TPU v7x, 32 devices: a whole 2x2x4 slice. The times are simulated.
32 devices in a mesh: ap: 16 (over z, x, core), pass: 2 (over y).
Axes of the slice: x: 2, y: 2, z: 4, core: 2. Of those that a mesh axis runs over, the one named last changes fastest.
Arguments:
- echo_record: bfloat16 [2, 16, 2048, 512], P(None, 'pass', 'ap'), may hold values from -6 to 6
- along_track_kernel: bfloat16 [2, 1024, 2048], P(None, None, 'ap'), may hold values from -0.125 to 0.125
- slant_distance_kernel: bfloat16 [2, 512, 256], replicated, may hold values from -0.1875 to 0.1875
- vertical_lags: int32 [16], P('pass'), may hold values from 0 to 128
- lateral_lags: int32 [16], P('pass'), may hold values from 0 to 32
- orbit_source_survey: int32 [16], replicated, may hold values from 0 to 15, each once
- normal_spacings: float32 [16], replicated, may hold values from -1 to 1
Outputs:
- profile: float32 [2, 1024, 256, 512], P(None, ('ap', 'pass'))
All inputs are finite; a program needn't handle non-finite values.
Results may differ from a plain program's by a relative error of at most 0.02.
Values may be sent and summed in bfloat16 or wider, within the bound.
A program may use at most 192 MiB of HBM per device.

v0:
```python
import jax
import jax.numpy as jnp
from jax import lax
from jax.sharding import PartitionSpec as P

HEIGHT_CELLS = 512
ITERS = 4
SPAN = 2
COL_MAX = 32


shrink_level = 0.1


def phasor_dictionary(normal_spacings, orbit_source_survey, height_cell_number):
    support_mask = (
        orbit_source_survey[:, None]
        == jnp.arange(normal_spacings.shape[0], dtype=jnp.int32)[None, :]
    ).astype(normal_spacings.dtype)
    chosen_height_cells = jnp.sum(support_mask * normal_spacings[None, :], axis=1)
    orbit_start_positions = (
        jnp.arange(height_cell_number).astype(normal_spacings.dtype) - height_cell_number // 2
    )
    phases = jnp.pi * chosen_height_cells[:, None] * orbit_start_positions[None, :]
    return (jnp.cos(phases), jnp.sin(phases))


def shrink_steps(obs_re, obs_im, inphase_phasor_part, quadrature_phasor_part):
    passes = inphase_phasor_part.shape[0]
    height_cell_number = inphase_phasor_part.shape[1]
    precise = lax.Precision.HIGHEST
    prof_re = jnp.zeros((obs_re.shape[0], height_cell_number), jnp.float32)
    prof_im = jnp.zeros((obs_re.shape[0], height_cell_number), jnp.float32)
    for sweep_index in range(ITERS):
        if sweep_index == 0:
            resid_re = obs_re
            resid_im = obs_im
        else:
            pred_re = jnp.dot(prof_re, inphase_phasor_part.T, precision=precise) - jnp.dot(
                prof_im, quadrature_phasor_part.T, precision=precise
            )
            pred_im = jnp.dot(prof_re, quadrature_phasor_part.T, precision=precise) + jnp.dot(
                prof_im, inphase_phasor_part.T, precision=precise
            )
            resid_re = obs_re - pred_re / height_cell_number
            resid_im = obs_im - pred_im / height_cell_number
        grad_re = jnp.dot(resid_re, inphase_phasor_part, precision=precise) + jnp.dot(
            resid_im, quadrature_phasor_part, precision=precise
        )
        grad_im = jnp.dot(resid_im, inphase_phasor_part, precision=precise) - jnp.dot(
            resid_re, quadrature_phasor_part, precision=precise
        )
        moved_re = prof_re + grad_re / passes
        moved_im = prof_im + grad_im / passes
        prof_re = moved_re - jnp.clip(moved_re, -shrink_level, shrink_level)
        prof_im = moved_im - jnp.clip(moved_im, -shrink_level, shrink_level)
    return (prof_re, prof_im)


def focus_range(echo_record, slant_distance_kernel):
    kernel_re, kernel_im = (slant_distance_kernel[0], slant_distance_kernel[1])
    focus_re = jnp.einsum(
        "ptf,fc->ptc", echo_record[0], kernel_re, preferred_element_type=jnp.float32
    ) - jnp.einsum("ptf,fc->ptc", echo_record[1], kernel_im, preferred_element_type=jnp.float32)
    focus_im = jnp.einsum(
        "ptf,fc->ptc", echo_record[0], kernel_im, preferred_element_type=jnp.float32
    ) + jnp.einsum("ptf,fc->ptc", echo_record[1], kernel_re, preferred_element_type=jnp.float32)
    return (focus_re.astype(jnp.bfloat16), focus_im.astype(jnp.bfloat16))


def azimuth_terms(kernel_re, kernel_im, focus_re, focus_im):
    pattern = "prt,ptc->prc"
    image_re = jnp.einsum(
        pattern, kernel_re, focus_re, preferred_element_type=jnp.float32
    ) - jnp.einsum(pattern, kernel_im, focus_im, preferred_element_type=jnp.float32)
    image_im = jnp.einsum(
        pattern, kernel_re, focus_im, preferred_element_type=jnp.float32
    ) + jnp.einsum(pattern, kernel_im, focus_re, preferred_element_type=jnp.float32)
    return (image_re, image_im)


def shift_kernel(kernel, vertical_lags, margin):
    padded = jnp.pad(kernel, ((0, 0), (margin, 0), (0, 0)))

    def choose_rows(offset):
        return lax.dynamic_slice_in_dim(padded, margin - offset, kernel.shape[1], 1)

    return jax.vmap(choose_rows, out_axes=1)(vertical_lags)


def shift_columns(image_block, lateral_lags):
    padded = jnp.pad(image_block, ((0, 0), (0, 0), (0, 0), (COL_MAX, 0)))

    def choose_cols(planes, offset):
        return lax.dynamic_slice_in_dim(planes, COL_MAX - offset, image_block.shape[3], 2)

    return jax.vmap(choose_cols, in_axes=(1, 0), out_axes=1)(padded, lateral_lags)


def body(
    echo_record,
    along_track_kernel,
    slant_distance_kernel,
    vertical_lags,
    lateral_lags,
    orbit_source_survey,
    normal_spacings,
):
    ap_count = lax.axis_size("ap")
    strip_height = along_track_kernel.shape[1] // ap_count
    focus_re, focus_im = focus_range(echo_record, slant_distance_kernel)
    kernel = shift_kernel(along_track_kernel, vertical_lags, SPAN * strip_height)
    image_re, image_im = azimuth_terms(kernel[0], kernel[1], focus_re, focus_im)
    image_block = lax.psum_scatter(
        jnp.stack([image_re, image_im]).astype(jnp.bfloat16), "ap", scatter_dimension=2, tiled=True
    ).astype(jnp.float32)
    aligned = shift_columns(image_block, lateral_lags).astype(jnp.bfloat16)
    inphase_phasor_part, quadrature_phasor_part = phasor_dictionary(
        normal_spacings, orbit_source_survey, HEIGHT_CELLS
    )
    stacked = lax.all_to_all(aligned, "pass", split_axis=2, concat_axis=1, tiled=True)
    row_count = stacked.shape[2]
    col_count = stacked.shape[3]
    flattened = stacked.astype(jnp.float32).reshape(2, stacked.shape[1], row_count * col_count)
    prof_re, prof_im = shrink_steps(
        flattened[0].T, flattened[1].T, inphase_phasor_part, quadrature_phasor_part
    )
    return jnp.stack([prof_re, prof_im]).reshape(
        2, row_count, col_count, inphase_phasor_part.shape[1]
    )


def solution(mesh):
    return jax.shard_map(
        body,
        mesh=mesh,
        in_specs=(
            P(None, "pass", "ap", None),
            P(None, None, "ap"),
            P(),
            P("pass"),
            P("pass"),
            P(),
            P(),
        ),
        out_specs=P(None, ("ap", "pass"), None, None),
        check_vma=False,
    )
```

profile of v0, /device:TPU:0, one launch (start us, length us, event | category | flops | bytes accessed | tf_op | source)
XLA Modules:
  0.0 683.9 jit_solution(11449470942167369225)
XLA Ops:
  16.5 16.7 %while.1 = (s32[]{:T(128)}, bf16[2,1152,128]{2,1,0:T(8,128)(2,1)S(1)}, s32[8,3]{0,1:T(4,128)S(1)}, bf16[8,2,1024,128]{3,2,0,1:T(8,128)(2,1)}, s32[]{:T(128)}) while((s32[]{:T(128)}, bf16[2,1152,128]{2,1,0:T(8,128)(2,1)S(1)}, s32[8,3]{0,1:T(4,128)S(1)}, bf16[8,2,1024,128]{3,2,0,1:T(8,128)(2,1)}, s32[]{:T(128)}) %tuple.19), condition=%wide.while_cond, body=%wide.while_body.sunk | while | flops 2 | bytes 1049197 | solution.py:86
  50.1 106.4 %reduce-scatter.2.cloned.1.call-done = bf16[2,8,64,256]{3,2,1,0:T(8,128)(2,1)} async-done(((bf16[2,8,1024,256]{3,2,1,0:T(8,128)(2,1)}), bf16[2,8,64,256]{3,2,1,0:T(8,128)(2,1)}) %reduce-scatter.2.cloned.1.call-update) | async-done | bytes 524304 | tf_op jit(solution)/shard_map/reduce_scatter | solution.py:114
  167.6 7.8 %all-to-all-done = bf16[2,8,64,256]{3,1,0,2:T(8,128)(2,1)S(1)} async-done(((bf16[2,8,64,256]{3,1,0,2:T(8,128)(2,1)}), bf16[2,8,64,256]{3,1,0,2:T(8,128)(2,1)S(1)}, u32[]{:S(2)}, u32[]{:S(2)}) %all-to-all-start) | async-done | bytes 524320 | tf_op jit(solution)/shard_map/all_to_all | solution.py:121
  176.1 10.6 %fusion.46 = f32[8192,512]{1,0:T(8,128)} fusion(bf16[16,8192]{1,0:T(8,128)(2,1)S(1)} %bitcast.122, f32[512]{0:T(512)S(1)} %convert_add_fusion, f32[16]{0:T(128)S(1)} %broadcast_multiply_fusion), kind=kOutput, calls=%fused_computation.77 | convolution fusion | flops 805314560 | bytes 17041472 | tf_op jit(solution)/shard_map/dot_general | solution.py:47
  186.6 12.4 %clamp_subtract_fusion.7 = f32[8192,512]{1,0:T(8,128)S(1)} fusion(f32[8192,512]{1,0:T(8,128)} %fusion.46, bf16[16,8192]{1,0:T(8,128)(2,1)S(1)} %bitcast.124, f32[512]{0:T(512)S(1)} %convert_add_fusion, f32[16]{0:T(128)S(1)} %broadcast_multiply_fusion), kind=kOutput, calls=%fused_computation.11 | convolution fusion | flops 822091776 | bytes 33818688 | tf_op jit(solution)/shard_map/dot_general | solution.py:47
  199.1 14.3 %fusion.49 = f32[8192,16]{0,1:T(8,128)S(1)} fusion(f32[8192,512]{1,0:T(8,128)S(1)} %clamp_subtract_fusion.7, f32[512]{0:T(512)S(1)} %convert_add_fusion, f32[16]{0:T(128)S(1)} %broadcast_multiply_fusion), kind=kOutput, calls=%fused_computation.80 | convolution fusion | flops 805314560 | bytes 17303616 | tf_op jit(solution)/shard_map/dot_general | solution.py:42
  213.4 14.8 %fusion.45 = f32[8192,16]{0,1:T(8,128)S(1)} fusion(f32[8192,512]{1,0:T(8,128)S(1)} %clamp_subtract_fusion.7, f32[512]{0:T(512)S(1)} %convert_add_fusion, f32[16]{0:T(128)S(1)} %broadcast_multiply_fusion), kind=kOutput, calls=%fused_computation.76 | convolution fusion | flops 805314560 | bytes 17303616 | tf_op jit(solution)/shard_map/dot_general | solution.py:39
  228.2 10.6 %fusion.44 = f32[8192,512]{1,0:T(8,128)} fusion(bf16[16,8192]{1,0:T(8,128)(2,1)S(1)} %bitcast.125, f32[512]{0:T(512)S(1)} %convert_add_fusion, f32[16]{0:T(128)S(1)} %broadcast_multiply_fusion), kind=kOutput, calls=%fused_computation.75 | convolution fusion | flops 805314560 | bytes 17041472 | tf_op jit(solution)/shard_map/dot_general | solution.py:50
  239.4 12.2 %clamp_subtract_fusion.6 = f32[8192,512]{1,0:T(8,128)S(1)} fusion(f32[8192,512]{1,0:T(8,128)} %fusion.44, bf16[16,8192]{1,0:T(8,128)(2,1)S(1)} %bitcast.123, f32[512]{0:T(512)S(1)} %convert_add_fusion, f32[16]{0:T(128)S(1)} %broadcast_multiply_fusion), kind=kOutput, calls=%fused_computation.10 | convolution fusion | flops 822091776 | bytes 33818688 | tf_op jit(solution)/shard_map/dot_general | solution.py:50
  251.6 14.3 %fusion.6 = f32[8192,16]{0,1:T(8,128)S(1)} fusion(f32[8192,16]{0,1:T(8,128)S(1)} %bitcast.110, f32[8192,16]{0,1:T(8,128)S(1)} %fusion.45, f32[8192,512]{1,0:T(8,128)S(1)} %clamp_subtract_fusion.6, f32[512]{0:T(512)S(1)} %convert_add_fusion, f32[16]{0:T(128)S(1)} %broadcast_multiply_fusion), kind=kOutput, calls=%fused_computation.24 | convolution fusion | flops 805707776 | bytes 18352192 | tf_op jit(solution)/shard_map/dot_general | solution.py:39
  265.9 16.6 %fusion.43 = f32[8192,512]{1,0:T(8,128)} fusion(f32[8192,16]{0,1:T(8,128)S(1)} %fusion.6, f32[512]{0:T(512)S(1)} %convert_add_fusion, f32[16]{0:T(128)S(1)} %broadcast_multiply_fusion), kind=kOutput, calls=%fused_computation.74 | convolution fusion | flops 805314560 | bytes 17303616 | tf_op jit(solution)/shard_map/dot_general | solution.py:47
  282.6 14.5 %fusion.7 = f32[8192,16]{0,1:T(8,128)S(1)} fusion(f32[8192,16]{0,1:T(8,128)S(1)} %bitcast.113, f32[8192,16]{0,1:T(8,128)S(1)} %fusion.49, f32[8192,512]{1,0:T(8,128)S(1)} %clamp_subtract_fusion.6, f32[512]{0:T(512)S(1)} %convert_add_fusion, f32[16]{0:T(128)S(1)} %broadcast_multiply_fusion), kind=kOutput, calls=%fused_computation.25 | convolution fusion | flops 805707776 | bytes 18352192 | tf_op jit(solution)/shard_map/dot_general | solution.py:42
  297.1 22.7 %clamp_subtract_fusion.5 = f32[8192,512]{1,0:T(8,128)} fusion(f32[8192,512]{1,0:T(8,128)} %copy-done, f32[8192,512]{1,0:T(8,128)} %fusion.43, f32[8192,16]{0,1:T(8,128)S(1)} %fusion.7, f32[512]{0:T(512)S(1)} %convert_add_fusion, f32[16]{0:T(128)S(1)} %broadcast_multiply_fusion), kind=kOutput, calls=%fused_computation.9 | convolution fusion | flops 826286080 | bytes 50858048 | tf_op jit(solution)/shard_map/dot_general | solution.py:47
  319.8 19.9 %fusion.48 = f32[8192,16]{0,1:T(8,128)S(1)} fusion(f32[8192,512]{1,0:T(8,128)} %clamp_subtract_fusion.5, f32[512]{0:T(512)S(1)} %convert_add_fusion, f32[16]{0:T(128)S(1)} %broadcast_multiply_fusion), kind=kOutput, calls=%fused_computation.79 | convolution fusion | flops 805314560 | bytes 17303616 | tf_op jit(solution)/shard_map/dot_general | solution.py:42
  339.7 14.7 %fusion.42 = f32[8192,16]{0,1:T(8,128)S(1)} fusion(f32[8192,512]{1,0:T(8,128)S(1)} %copy-done.2, f32[512]{0:T(512)S(1)} %convert_add_fusion, f32[16]{0:T(128)S(1)} %broadcast_multiply_fusion), kind=kOutput, calls=%fused_computation.73 | convolution fusion | flops 805314560 | bytes 17303616 | tf_op jit(solution)/shard_map/dot_general | solution.py:39
  354.4 16.3 %fusion.41 = f32[8192,512]{1,0:T(8,128)} fusion(f32[8192,16]{0,1:T(8,128)S(1)} %fusion.7, f32[512]{0:T(512)S(1)} %convert_add_fusion, f32[16]{0:T(128)S(1)} %broadcast_multiply_fusion), kind=kOutput, calls=%fused_computation.72 | convolution fusion | flops 805314560 | bytes 17303616 | tf_op jit(solution)/shard_map/dot_general | solution.py:50
  370.7 22.8 %clamp_subtract_fusion.4 = f32[8192,512]{1,0:T(8,128)} fusion(f32[8192,512]{1,0:T(8,128)} %copy-done.3, f32[8192,512]{1,0:T(8,128)} %fusion.41, f32[8192,16]{0,1:T(8,128)S(1)} %fusion.6, f32[512]{0:T(512)S(1)} %convert_add_fusion, f32[16]{0:T(128)S(1)} %broadcast_multiply_fusion), kind=kOutput, calls=%fused_computation.8 | convolution fusion | flops 826286080 | bytes 50858048 | tf_op jit(solution)/shard_map/dot_general | solution.py:50
  393.5 19.9 %fusion.9 = f32[8192,16]{0,1:T(8,128)S(1)} fusion(f32[8192,16]{0,1:T(8,128)S(1)} %bitcast.114, f32[8192,16]{0,1:T(8,128)S(1)} %fusion.48, f32[8192,512]{1,0:T(8,128)} %clamp_subtract_fusion.4, f32[512]{0:T(512)S(1)} %convert_add_fusion, f32[16]{0:T(128)S(1)} %broadcast_multiply_fusion), kind=kOutput, calls=%fused_computation.27 | convolution fusion | flops 805707776 | bytes 18352192 | tf_op jit(solution)/shard_map/dot_general | solution.py:42
  413.4 14.3 %fusion.8 = f32[8192,16]{0,1:T(8,128)S(1)} fusion(f32[8192,16]{0,1:T(8,128)S(1)} %bitcast.111, f32[8192,16]{0,1:T(8,128)S(1)} %fusion.42, f32[8192,512]{1,0:T(8,128)S(1)} %copy-done.5, f32[512]{0:T(512)S(1)} %convert_add_fusion, f32[16]{0:T(128)S(1)} %broadcast_multiply_fusion), kind=kOutput, calls=%fused_computation.26 | convolution fusion | flops 805707776 | bytes 18352192 | tf_op jit(solution)/shard_map/dot_general | solution.py:39
  427.7 16.7 %fusion.40 = f32[8192,512]{1,0:T(8,128)} fusion(f32[8192,16]{0,1:T(8,128)S(1)} %fusion.8, f32[512]{0:T(512)S(1)} %convert_add_fusion, f32[16]{0:T(128)S(1)} %broadcast_multiply_fusion), kind=kOutput, calls=%fused_computation.71 | convolution fusion | flops 805314560 | bytes 17303616 | tf_op jit(solution)/shard_map/dot_general | solution.py:47
  444.4 22.7 %clamp_subtract_fusion.3 = f32[8192,512]{1,0:T(8,128)} fusion(f32[8192,512]{1,0:T(8,128)} %clamp_subtract_fusion.5, f32[8192,512]{1,0:T(8,128)} %fusion.40, f32[8192,16]{0,1:T(8,128)S(1)} %fusion.9, f32[512]{0:T(512)S(1)} %convert_add_fusion, f32[16]{0:T(128)S(1)} %broadcast_multiply_fusion), kind=kOutput, calls=%fused_computation.7 | convolution fusion | flops 826286080 | bytes 50858048 | tf_op jit(solution)/shard_map/dot_general | solution.py:47
  467.1 19.8 %fusion.47 = f32[8192,16]{0,1:T(8,128)S(1)} fusion(f32[8192,512]{1,0:T(8,128)} %clamp_subtract_fusion.3, f32[512]{0:T(512)S(1)} %convert_add_fusion, f32[16]{0:T(128)S(1)} %broadcast_multiply_fusion), kind=kOutput, calls=%fused_computation.78 | convolution fusion | flops 805314560 | bytes 17303616 | tf_op jit(solution)/shard_map/dot_general | solution.py:42
  486.9 14.7 %fusion.39 = f32[8192,16]{0,1:T(8,128)S(1)} fusion(f32[8192,512]{1,0:T(8,128)S(1)} %copy-done.1, f32[512]{0:T(512)S(1)} %convert_add_fusion, f32[16]{0:T(128)S(1)} %broadcast_multiply_fusion), kind=kOutput, calls=%fused_computation.70 | convolution fusion | flops 805314560 | bytes 17303616 | tf_op jit(solution)/shard_map/dot_general | solution.py:39
  501.6 16.3 %fusion.38 = f32[8192,512]{1,0:T(8,128)} fusion(f32[8192,16]{0,1:T(8,128)S(1)} %fusion.9, f32[512]{0:T(512)S(1)} %convert_add_fusion, f32[16]{0:T(128)S(1)} %broadcast_multiply_fusion), kind=kOutput, calls=%fused_computation.69 | convolution fusion | flops 805314560 | bytes 17303616 | tf_op jit(solution)/shard_map/dot_general | solution.py:50
  517.8 22.8 %clamp_subtract_fusion.2 = f32[8192,512]{1,0:T(8,128)} fusion(f32[8192,512]{1,0:T(8,128)} %clamp_subtract_fusion.4, f32[8192,512]{1,0:T(8,128)} %fusion.38, f32[8192,16]{0,1:T(8,128)S(1)} %fusion.8, f32[512]{0:T(512)S(1)} %convert_add_fusion, f32[16]{0:T(128)S(1)} %broadcast_multiply_fusion), kind=kOutput, calls=%fused_computation.6 | convolution fusion | flops 826286080 | bytes 50858048 | tf_op jit(solution)/shard_map/dot_general | solution.py:50
  540.6 19.9 %fusion.11 = f32[8192,16]{0,1:T(8,128)S(1)} fusion(f32[8192,16]{0,1:T(8,128)S(1)} %bitcast.115, f32[8192,16]{0,1:T(8,128)S(1)} %fusion.47, f32[8192,512]{1,0:T(8,128)} %clamp_subtract_fusion.2, f32[512]{0:T(512)S(1)} %convert_add_fusion, f32[16]{0:T(128)S(1)} %broadcast_multiply_fusion), kind=kOutput, calls=%fused_computation.29 | convolution fusion | flops 805707776 | bytes 18352192 | tf_op jit(solution)/shard_map/dot_general | solution.py:42
  560.6 14.3 %fusion.10 = f32[8192,16]{0,1:T(8,128)S(1)} fusion(f32[8192,16]{0,1:T(8,128)S(1)} %bitcast.112, f32[8192,16]{0,1:T(8,128)S(1)} %fusion.39, f32[8192,512]{1,0:T(8,128)S(1)} %copy-done.4, f32[512]{0:T(512)S(1)} %convert_add_fusion, f32[16]{0:T(128)S(1)} %broadcast_multiply_fusion), kind=kOutput, calls=%fused_computation.28 | convolution fusion | flops 805707776 | bytes 18352192 | tf_op jit(solution)/shard_map/dot_general | solution.py:39
  574.9 16.5 %fusion.37 = f32[8192,512]{1,0:T(8,128)} fusion(f32[8192,16]{0,1:T(8,128)S(1)} %fusion.10, f32[512]{0:T(512)S(1)} %convert_add_fusion, f32[16]{0:T(128)S(1)} %broadcast_multiply_fusion), kind=kOutput, calls=%fused_computation.68 | convolution fusion | flops 805314560 | bytes 17303616 | tf_op jit(solution)/shard_map/dot_general | solution.py:47
  591.3 16.3 %fusion.36 = f32[8192,512]{1,0:T(8,128)} fusion(f32[8192,16]{0,1:T(8,128)S(1)} %fusion.11, f32[512]{0:T(512)S(1)} %convert_add_fusion, f32[16]{0:T(128)S(1)} %broadcast_multiply_fusion), kind=kOutput, calls=%fused_computation.67 | convolution fusion | flops 805314560 | bytes 17303616 | tf_op jit(solution)/shard_map/dot_general | solution.py:50
  607.6 22.7 %clamp_subtract_fusion.1 = f32[8192,512]{1,0:T(8,128)} fusion(f32[8192,512]{1,0:T(8,128)} %clamp_subtract_fusion.3, f32[8192,512]{1,0:T(8,128)} %fusion.37, f32[8192,16]{0,1:T(8,128)S(1)} %fusion.11, f32[512]{0:T(512)S(1)} %convert_add_fusion, f32[16]{0:T(128)S(1)} %broadcast_multiply_fusion), kind=kOutput, calls=%fused_computation.5 | convolution fusion | flops 826286080 | bytes 50858048 | tf_op jit(solution)/shard_map/dot_general | solution.py:47
  630.3 22.9 %clamp_subtract_fusion = f32[8192,512]{1,0:T(8,128)} fusion(f32[8192,512]{1,0:T(8,128)} %clamp_subtract_fusion.2, f32[8192,512]{1,0:T(8,128)} %fusion.36, f32[8192,16]{0,1:T(8,128)S(1)} %fusion.10, f32[512]{0:T(512)S(1)} %convert_add_fusion, f32[16]{0:T(128)S(1)} %broadcast_multiply_fusion), kind=kOutput, calls=%fused_computation.4 | convolution fusion | flops 826286080 | bytes 50858048 | tf_op jit(solution)/shard_map/dot_general | solution.py:50
  653.2 23.4 %pad_maximum_fusion = f32[2,32,256,512]{3,2,1,0:T(8,128)} fusion(f32[1,32,256,512]{3,2,1,0:T(8,128)} %bitcast.109, f32[1,32,256,512]{3,2,1,0:T(8,128)} %bitcast.108), kind=kLoop, calls=%fused_computation.3 | loop fusion | flops 8388608 | bytes 67108864 | tf_op jit(solution)/shard_map/stack | solution.py:128
  (77 shorter events, 55.8 us)
Async XLA Ops:
  6.5 149.9 %reduce-scatter.2.cloned.1.call-start = ((), (), s32[]{:S(2)}) async-start(), calls=%async_computation.2 | async-start | bytes 8912896 | tf_op jit(solution)/shard_map/reduce_scatter | solution.py:114
  33.2 5.8 copy-start.6
  40.3 9.6 %copy-start.7 = (f32[16]{0:T(128)S(1)}, f32[16]{0:T(128)}, u32[]{:S(2)}) copy-start(f32[16]{0:T(128)} %param.13) | copy-start | bytes 196
  40.3 9.6 %copy-start.8 = (s32[16]{0:T(128)S(1)}, s32[16]{0:T(128)}, u32[]{:S(2)}) copy-start(s32[16]{0:T(128)} %param.12) | copy-start | bytes 196
  40.3 9.8 %copy-start.9 = (s32[8]{0:T(128)S(1)}, s32[8]{0:T(128)}, u32[]{:S(2)}) copy-start(s32[8]{0:T(128)} %param.11) | copy-start | bytes 100
  163.8 11.6 %all-to-all-start = ((bf16[2,8,64,256]{3,1,0,2:T(8,128)(2,1)}), bf16[2,8,64,256]{3,1,0,2:T(8,128)(2,1)S(1)}, u32[]{:S(2)}, u32[]{:S(2)}) async-start(bf16[2,8,64,256]{3,1,0,2:T(8,128)(2,1)} %copy.33), calls=%async_computation.1 | async-start | bytes 1048576 | tf_op jit(solution)/shard_map/all_to_all | solution.py:121
  199.1 29.1 %copy-start = (f32[8192,512]{1,0:T(8,128)}, f32[8192,512]{1,0:T(8,128)S(1)}, u32[]{:S(2)}) copy-start(f32[8192,512]{1,0:T(8,128)S(1)} %clamp_subtract_fusion.7) | copy-start | bytes 50331652
  251.6 31.0 %copy-start.3 = (f32[8192,512]{1,0:T(8,128)}, f32[8192,512]{1,0:T(8,128)S(1)}, u32[]{:S(2)}) copy-start(f32[8192,512]{1,0:T(8,128)S(1)} %clamp_subtract_fusion.6) | copy-start | bytes 50331652
  319.8 19.9 %copy-start.2 = (f32[8192,512]{1,0:T(8,128)S(1)}, f32[8192,512]{1,0:T(8,128)}, u32[]{:S(2)}) copy-start(f32[8192,512]{1,0:T(8,128)} %clamp_subtract_fusion.5) | copy-start | bytes 50331652
  393.5 19.9 %copy-start.5 = (f32[8192,512]{1,0:T(8,128)S(1)}, f32[8192,512]{1,0:T(8,128)}, u32[]{:S(2)}) copy-start(f32[8192,512]{1,0:T(8,128)} %clamp_subtract_fusion.4) | copy-start | bytes 50331652
  467.1 19.8 %copy-start.1 = (f32[8192,512]{1,0:T(8,128)S(1)}, f32[8192,512]{1,0:T(8,128)}, u32[]{:S(2)}) copy-start(f32[8192,512]{1,0:T(8,128)} %clamp_subtract_fusion.3) | copy-start | bytes 50331652
  540.6 19.9 %copy-start.4 = (f32[8192,512]{1,0:T(8,128)S(1)}, f32[8192,512]{1,0:T(8,128)}, u32[]{:S(2)}) copy-start(f32[8192,512]{1,0:T(8,128)} %clamp_subtract_fusion.2) | copy-start | bytes 50331652
Sparse Core Ops, SparseCore 0:
  50.0 106.4 reduce-scatter.1
where the time goes:
time: 692 us; the launch traced here: 684 us
  matrix products  495 us (72%)
  waiting for transfers between devices  114 us (16%)
  other arithmetic  30.6 us (4%)
  local copies, waits for them, and re-layouts  26.5 us (4%)
  between operations  14.2 us (2%)
    reduce_scatter x1, waiting for transfers between devices, body(): lax.psum_scatter(jnp.stack([image_re, image_im]).astype(jnp.bfloat16), 'a...  106 us
    dot_general x4, matrix products, shrink_steps(): jnp.dot(resid_re, quadrature_phasor_part, precision=precise)  80.7 us
    dot_general x4, matrix products, shrink_steps(): jnp.dot(resid_im, quadrature_phasor_part, precision=precise)  80.5 us
    dot_general x4, matrix products, shrink_steps(): jnp.dot(resid_re, inphase_phasor_part, precision=precise)  60.4 us
    dot_general x4, matrix products, shrink_steps(): jnp.dot(resid_im, inphase_phasor_part, precision=precise)  59.4 us
    dot_general x3, matrix products, shrink_steps(): jnp.dot(prof_im, inphase_phasor_part.T, precision=precise)  54.3 us
    dot_general x3, matrix products, shrink_steps(): jnp.dot(prof_re, quadrature_phasor_part.T, precision=precise)  54 us
    dot_general x3, matrix products, shrink_steps(): jnp.dot(prof_re, inphase_phasor_part.T, precision=precise)  44.2 us
  transfers between devices with their start and end apart: 2, of which 2 were waited for; matrix products, arithmetic and copies ran while one was open for 0% of the time, Pallas kernels for 0%

commit v1 on v0

v1 whole, which is shorter than its diff:
```python
import functools

import jax
import jax.numpy as jnp
from jax import lax
from jax.experimental import pallas as pl
from jax.experimental.pallas import tpu as pltpu
from jax.sharding import PartitionSpec as P

HEIGHT_CELLS = 512
ITERS = 4
SPAN = 2
CHUNKS = 4
LANES = 256

shrink_level = 0.1


def phasor_dictionary(normal_spacings, orbit_source_survey, height_cell_number):
    support_mask = (
        orbit_source_survey[:, None]
        == jnp.arange(normal_spacings.shape[0], dtype=jnp.int32)[None, :]
    ).astype(normal_spacings.dtype)
    chosen_height_cells = jnp.sum(support_mask * normal_spacings[None, :], axis=1)
    orbit_start_positions = (
        jnp.arange(height_cell_number).astype(normal_spacings.dtype) - height_cell_number // 2
    )
    phases = jnp.pi * chosen_height_cells[:, None] * orbit_start_positions[None, :]
    return (jnp.cos(phases), jnp.sin(phases))


def focus_kernel(lags_ref, echo_ref, slant_ref, out_ref):
    dot = functools.partial(jnp.dot, preferred_element_type=jnp.float32)
    echo_re, echo_im = echo_ref[0, 0], echo_ref[1, 0]
    slant_re, slant_im = slant_ref[0], slant_ref[1]
    lag = lags_ref[pl.program_id(0)]
    focus_re = dot(echo_re, slant_re) - dot(echo_im, slant_im)
    focus_im = dot(echo_re, slant_im) + dot(echo_im, slant_re)
    inside = lax.broadcasted_iota(jnp.int32, focus_re.shape, 1) >= lag
    for plane, values in enumerate((focus_re, focus_im)):
        moved = jnp.where(inside, pltpu.roll(values, lag, 1), 0.0)
        out_ref[plane, 0] = moved.astype(out_ref.dtype)


def focus_range(echo, slant, lateral_lags):
    _, passes, pulses, freqs = echo.shape
    cols = slant.shape[2]
    return pl.pallas_call(
        focus_kernel,
        grid_spec=pltpu.PrefetchScalarGridSpec(
            num_scalar_prefetch=1,
            grid=(passes,),
            in_specs=[
                pl.BlockSpec((2, 1, pulses, freqs), lambda p, lags: (0, p, 0, 0)),
                pl.BlockSpec((2, freqs, cols), lambda p, lags: (0, 0, 0)),
            ],
            out_specs=pl.BlockSpec((2, 1, pulses, cols), lambda p, lags: (0, p, 0, 0)),
        ),
        out_shape=jax.ShapeDtypeStruct((2, passes, pulses, cols), jnp.bfloat16),
        cost_estimate=pl.CostEstimate(
            flops=8 * passes * pulses * freqs * cols,
            bytes_accessed=6 * passes * pulses * freqs,
            transcendentals=0,
        ),
        name="focus",
    )(lateral_lags, echo, slant)


def image_kernel(chunks, pass_count, strip, margin, lags_ref, side_ref, *refs):
    kernels, focuses = refs[0:2], refs[2:4]
    outs, padded = refs[4 : 4 + chunks], refs[4 + chunks]
    owners = outs[0].shape[0]
    rows = kernels[0].shape[1]
    pulses = kernels[0].shape[2]
    cols = outs[0].shape[4]

    @pl.when(pl.program_id(0) == 0)
    def _():
        for s in range(2):
            for plane in range(2):
                padded[2 * s + plane, 0:margin, :] = jnp.zeros((margin, pulses), jnp.float32)
                padded[2 * s + plane, margin : margin + rows, :] = kernels[s][plane].astype(
                    jnp.float32
                )

    base = margin - lags_ref[pl.program_id(0)] + side_ref[0] * strip
    total_re = jnp.zeros((owners * strip, cols), jnp.float32)
    total_im = jnp.zeros((owners * strip, cols), jnp.float32)
    dot = functools.partial(jnp.dot, preferred_element_type=jnp.float32)
    for s in range(2):
        kernel_re, kernel_im = (
            jnp.concatenate(
                [padded[2 * s + plane, pl.ds(base + 2 * o * strip, strip), :] for o in range(owners)],
                axis=0,
            ).astype(jnp.bfloat16)
            for plane in range(2)
        )
        focus_re, focus_im = focuses[s][0, 0], focuses[s][1, 0]
        if pulses % 128 == 0:
            both = jnp.concatenate([kernel_re, kernel_im], axis=1)
            total_re += dot(both, jnp.concatenate([focus_re, -focus_im], axis=0))
            total_im += dot(both, jnp.concatenate([focus_im, focus_re], axis=0))
        else:
            total_re += dot(kernel_re, focus_re) - dot(kernel_im, focus_im)
            total_im += dot(kernel_re, focus_im) + dot(kernel_im, focus_re)
    height = strip // pass_count // chunks
    for plane, total in enumerate((total_re, total_im)):
        if chunks == 1:
            outs[0][:, plane, 0] = total.reshape(owners, strip, cols).astype(jnp.bfloat16)
        else:
            split = total.reshape(owners, pass_count, chunks, height, cols)
            for c in range(chunks):
                outs[c][:, plane, 0] = (
                    split[:, :, c].reshape(owners, pass_count * height, cols).astype(jnp.bfloat16)
                )


def form_images(kernel, kernel_far, focus, focus_far, vertical_lags, side, chunks, pass_count, strip):
    _, rows, pulses = kernel.shape
    passes, cols = focus.shape[1], focus.shape[3]
    owners = rows // strip // 2
    margin = SPAN * strip
    piece = strip // chunks
    whole = pl.BlockSpec((2, rows, pulses), lambda p, *_: (0, 0, 0))
    one = pl.BlockSpec((2, 1, pulses, cols), lambda p, *_: (0, p, 0, 0))
    return pl.pallas_call(
        functools.partial(image_kernel, chunks, pass_count, strip, margin),
        grid_spec=pltpu.PrefetchScalarGridSpec(
            num_scalar_prefetch=2,
            grid=(passes,),
            in_specs=[whole, whole, one, one],
            out_specs=[
                pl.BlockSpec((owners, 2, 1, piece, cols), lambda p, *_: (0, 0, p, 0, 0))
            ]
            * chunks,
            scratch_shapes=[pltpu.VMEM((4, margin + rows, pulses), jnp.float32)],
        ),
        out_shape=[jax.ShapeDtypeStruct((owners, 2, passes, piece, cols), jnp.bfloat16)] * chunks,
        cost_estimate=pl.CostEstimate(
            flops=8 * passes * pulses * rows * cols,
            bytes_accessed=2 * passes * rows * cols,
            transcendentals=0,
        ),
        name="image",
    )(vertical_lags, side, kernel, kernel_far, focus, focus_far)


def shrink_kernel(rows_at_once, y_ref, grad_ref, pred_ref, *refs):
    out_ref = refs[-1]
    cells = out_ref.shape[3]
    cols = out_ref.shape[2]
    width = grad_ref.shape[0]
    block = width // 4
    dot = functools.partial(jnp.dot, preferred_element_type=jnp.float32)
    coarse = (lax.broadcasted_iota(jnp.int32, (cols, width), 1) // block) % 2 == 0
    places = [
        (plane, start) for plane in range(2) for start in range(0, cells, LANES)
    ]
    observed = []
    for i in range(rows_at_once):
        y = y_ref[:, i * cols : (i + 1) * cols].astype(jnp.float32)
        observed.append(jnp.concatenate([y] * 4, axis=0).T)
    resid = list(observed)
    for sweep in range(ITERS):
        for i in range(rows_at_once):
            high = resid[i].astype(jnp.bfloat16)
            low = (resid[i] - high.astype(jnp.float32)).astype(jnp.bfloat16)
            moving = jnp.where(coarse, high, low)
            pred = None
            for n, (plane, start) in enumerate(places):
                v = dot(moving, grad_ref[:, n * LANES : (n + 1) * LANES])
                if sweep > 0:
                    v += out_ref[plane, i, :, start : start + LANES]
                u = v - jnp.clip(v, -shrink_level, shrink_level)
                out_ref[plane, i, :, start : start + LANES] = u
                if sweep < ITERS - 1:
                    part = dot(
                        u.astype(jnp.bfloat16), pred_ref[n * LANES : (n + 1) * LANES, :]
                    )
                    pred = part if pred is None else pred + part
            if sweep < ITERS - 1:
                resid[i] = observed[i] - pred


def shrink_chunk(c, chunks, y, grad, pred, profile, shape):
    _, rows, cols, cells = shape
    height = rows // chunks
    rows_at_once = 2 if height % 2 == 0 else 1
    steps = height // rows_at_once
    width, span = grad.shape
    specs = [
        pl.BlockSpec((y.shape[0], rows_at_once * cols), lambda i: (0, i)),
        pl.BlockSpec((width, span), lambda i: (0, 0)),
        pl.BlockSpec((span, width), lambda i: (0, 0)),
    ]
    operands = [y, grad, pred]
    aliases = {}
    if profile is not None:
        specs.append(pl.BlockSpec(memory_space=pl.ANY))
        operands.append(profile)
        aliases = {3: 0}
    return pl.pallas_call(
        functools.partial(shrink_kernel, rows_at_once),
        grid=(steps,),
        in_specs=specs,
        out_specs=pl.BlockSpec(
            (2, rows_at_once, cols, cells), lambda i: (0, c * steps + i, 0, 0)
        ),
        out_shape=jax.ShapeDtypeStruct(shape, jnp.float32),
        input_output_aliases=aliases,
        cost_estimate=pl.CostEstimate(
            flops=7 * 2 * 8 * height * cols * span * LANES // 8,
            bytes_accessed=8 * height * cols * cells,
            transcendentals=0,
        ),
        name="shrink_%d" % c,
    )(*operands)


def split_high_low(matrix):
    high = matrix.astype(jnp.bfloat16)
    return high, (matrix - high.astype(jnp.float32)).astype(jnp.bfloat16)


def body(
    echo_record,
    along_track_kernel,
    slant_distance_kernel,
    vertical_lags,
    lateral_lags,
    orbit_source_survey,
    normal_spacings,
):
    ap_count = lax.axis_size("ap")
    pass_count = lax.axis_size("pass")
    rows = along_track_kernel.shape[1]
    cols = slant_distance_kernel.shape[2]
    strip = rows // ap_count
    own_rows = strip // pass_count
    chunks = max(1, min(CHUNKS, own_rows // 8))
    passes = normal_spacings.shape[0]
    swap = [(i, i ^ 1) for i in range(ap_count)]
    same_side = [[i for i in range(ap_count) if i % 2 == side] for side in range(2)]

    kernel_far = lax.ppermute(along_track_kernel, "ap", swap)
    focus = focus_range(echo_record, slant_distance_kernel, lateral_lags)
    focus_far = lax.ppermute(focus, "ap", swap)
    side = (lax.axis_index("ap") % 2).astype(jnp.int32).reshape(1)
    pieces = form_images(
        along_track_kernel, kernel_far, focus, focus_far, vertical_lags, side,
        chunks, pass_count, strip,
    )

    inphase, quadrature = phasor_dictionary(normal_spacings, orbit_source_survey, HEIGHT_CELLS)
    adjoint = (
        jnp.concatenate(
            [
                jnp.concatenate([inphase, -quadrature], axis=1),
                jnp.concatenate([quadrature, inphase], axis=1),
            ],
            axis=0,
        )
    )
    grad_high, grad_low = split_high_low(adjoint / passes)
    grad = jnp.concatenate([grad_high, grad_high, grad_low, grad_low], axis=0)
    forward = (adjoint.T / HEIGHT_CELLS).astype(jnp.bfloat16)
    pred = jnp.concatenate([forward] * 4, axis=1)

    profile = None
    shape = (2, own_rows, cols, HEIGHT_CELLS)
    arrived = []
    for piece in pieces:
        arrived.append(
            lax.all_to_all(
                piece, "ap", split_axis=0, concat_axis=0, axis_index_groups=same_side
            )
        )
    for c, received in enumerate(arrived):
        if profile is not None:
            received, profile = lax.optimization_barrier((received, profile))
        summed = jnp.sum(received.astype(jnp.float32), axis=0).astype(jnp.bfloat16)
        stacked = lax.all_to_all(summed, "pass", split_axis=2, concat_axis=1, tiled=True)
        y = stacked.reshape(2 * passes, -1)
        profile = shrink_chunk(c, chunks, y, grad, pred, profile, shape)
    return profile


def solution(mesh):
    return jax.shard_map(
        body,
        mesh=mesh,
        in_specs=(
            P(None, "pass", "ap", None),
            P(None, None, "ap"),
            P(),
            P("pass"),
            P("pass"),
            P(),
            P(),
        ),
        out_specs=P(None, ("ap", "pass"), None, None),
        check_vma=False,
    )
```

time: 692 us -> 187 us (0.27)
  matrix products: 495 us -> 0 us
  waiting for transfers between devices: 114 us -> 30.7 us
  Pallas kernels: 0 us -> 78.1 us
  blocking collectives: 0 us -> 53.7 us
  other arithmetic: 30.6 us -> 3.47 us
  local copies, waits for them, and re-layouts: 26.5 us -> 4.85 us
  between operations: 14.2 us -> 0.11 us
  starting transfers between devices: 3.7 us -> 14.8 us
    dot_general x36 -> x0, matrix products: 495 us -> none  [the longest x4 80.7 us: shrink_steps(): jnp.dot(resid_re, quadrature_phasor_part, precision=precise)]
    reduce_scatter x1 -> x0, waiting for transfers between devices: 106 us -> none  [body(): lax.psum_scatter(jnp.stack([image_re, image_im]).astype(jnp.bfloat16), 'a...]
    pallas_call x0 -> x6, Pallas kernels: none -> 78.1 us  [the longest x4 61.3 us: shrink_chunk(): pl.pallas_call(functools.partial(shrink_kernel, rows_at_once), grid=(step...]
    all_to_all x0 -> x4, blocking collectives: none -> 53.7 us  [the longest x1 33.2 us: body(): lax.all_to_all(piece, 'ap', split_axis=0, concat_axis=0, axis_index_group...]
    another operation x2 -> x0, other arithmetic: 29.7 us -> none  [the longest x1 23.4 us: body(): jnp.stack([prof_re, prof_im])]
    gather x25 -> x0, local copies, waits for them, and re-layouts: 20 us -> none
    all_to_all x1 -> x4, waiting for transfers between devices: 7.82 us -> 27.4 us  [the longest x3 23.8 us: body(): lax.all_to_all(piece, 'ap', split_axis=0, concat_axis=0, axis_index_group...]
    all_to_all x1 -> x4, starting transfers between devices: 3.7 us -> 14.3 us  [the longest x3 10.9 us: body(): lax.all_to_all(piece, 'ap', split_axis=0, concat_axis=0, axis_index_group...]
  transfers between devices with their start and end apart: 2 -> 6, of which waited for: 2 -> 5; matrix products, arithmetic and copies ran while one was open for 0% -> 3% of each run, Pallas kernels for 0% -> 25%
where the time goes in v1:
time: 187 us; the launch traced here: 186 us
  Pallas kernels  78.1 us (42%)
  blocking collectives  53.7 us (29%)
  waiting for transfers between devices  30.7 us (16%)
  starting transfers between devices  14.8 us (8%)
  local copies, waits for them, and re-layouts  4.85 us (3%)
  other arithmetic  3.47 us (2%)
    pallas_call x4, Pallas kernels, shrink_chunk(): pl.pallas_call(functools.partial(shrink_kernel, rows_at_once), grid=(step...  61.3 us
    all_to_all x1, blocking collectives, body(): lax.all_to_all(piece, 'ap', split_axis=0, concat_axis=0, axis_index_group...  33.2 us
    all_to_all x3, waiting for transfers between devices, body(): lax.all_to_all(piece, 'ap', split_axis=0, concat_axis=0, axis_index_group...  23.8 us
    all_to_all x3, blocking collectives, body(): lax.all_to_all(summed, 'pass', split_axis=2, concat_axis=1, tiled=True)  20.5 us
    all_to_all x3, starting transfers between devices, body(): lax.all_to_all(piece, 'ap', split_axis=0, concat_axis=0, axis_index_group...  10.9 us
    pallas_call x1, Pallas kernels, form_images(): pl.pallas_call(functools.partial(image_kernel, chunks, pass_count, strip,...  9.03 us
    pallas_call x1, Pallas kernels, focus_range(): pl.pallas_call(focus_kernel, grid_spec=pltpu.PrefetchScalarGridSpec(num_s...  7.72 us
  transfers between devices with their start and end apart: 6, of which 5 were waited for; matrix products, arithmetic and copies ran while one was open for 3% of the time, Pallas kernels for 25%

profile of v1, /device:TPU:0, one launch (start us, length us, event | category | flops | bytes accessed | tf_op | source)
XLA Modules:
  0.0 185.7 jit_solution(4446518799449004226)
XLA Ops:
  0.0 7.7 %focus.1.refs_2_ = bf16[2,8,128,256]{3,2,1,0:T(8,128)(2,1)} custom-call(s32[8]{0:T(128)} %lags_ref.2, bf16[2,8,128,512]{3,2,1,0:T(8,128)(2,1)} %echo_ref.1, bf16[2,512,256]{2,1,0:T(8,128)(2,1)} %slant_ref.1), custom_call_target="tpu_custom_call" | custom-call | flops 1073741824 | bytes 3145728 | tf_op jit(solution)/shard_map/focus/pallas_call | solution.py:48
  7.7 0.5 collective-permute-start.1
  8.2 3.2 %collective-permute-done.refs_1_ = bf16[2,1024,128]{2,1,0:T(8,128)(2,1)S(1)} collective-permute-done((bf16[2,1024,128]{2,1,0:T(8,128)(2,1)}, bf16[2,1024,128]{2,1,0:T(8,128)(2,1)S(1)}, u32[]{:S(2)}, u32[]{:S(2)}) %collective-permute-start) | collective-permute-done | bytes 524320 | tf_op jit(solution)/shard_map/ppermute | solution.py:245
  11.5 0.8 copy-done.1
  12.3 0.4 copy-done
  12.6 9.0 %image.1 = (bf16[8,2,8,16,256]{4,3,2,1,0:T(8,128)(2,1)}, bf16[8,2,8,16,256]{4,3,2,1,0:T(8,128)(2,1)}, bf16[8,2,8,16,256]{4,3,2,1,0:T(8,128)(2,1)}, bf16[8,2,8,16,256]{4,3,2,1,0:T(8,128)(2,1)}) custom-call(s32[8]{0:T(128)} %lags_ref.3, s32[1]{0:T(128)} %bitcast.side_ref, bf16[2,1024,128]{2,1,0:T(8,128)(2,1)} %refs_0_.1, bf16[2,1024,128]{2,1,0:T(8,128)(2,1)} %copy-done.1, ...), custom_call_target="tpu_custom_call" | custom-call | flops 2147483648 | bytes 4194304 | tf_op jit(solution)/shard_map/image/pallas_call | solution.py:126
  21.7 33.2 %all_to_all.80 = bf16[8,2,8,16,256]{4,3,2,1,0:T(8,128)(2,1)S(1)} all-to-all(bf16[8,2,8,16,256]{4,3,2,1,0:T(8,128)(2,1)} %get-tuple-element.18), channel_id=1, replica_groups={{0,4,8,12,16,20,24,28},{2,6,10,14,18,22,26,30},{1,5,9,13,17,21,25,29},{..., dimensions={0} | all-to-all | bytes 2097152 | tf_op jit(solution)/shard_map/all_to_all | solution.py:274
  55.0 0.7 copy.33
  55.7 3.4 %all-to-all-start.4 = ((bf16[2,8,16,256]{3,1,0,2:T(8,128)(2,1)}), bf16[2,8,16,256]{3,1,0,2:T(8,128)(2,1)S(1)}, u32[]{:S(2)}, u32[]{:S(2)}) async-start(bf16[2,8,16,256]{3,1,0,2:T(8,128)(2,1)} %copy.33), calls=%async_computation.4 | async-start | bytes 262144 | tf_op jit(solution)/shard_map/all_to_all | solution.py:282
  59.1 0.9 select_reduce_fusion
  59.9 3.6 %all-to-all-done.4 = bf16[2,8,16,256]{3,1,0,2:T(8,128)(2,1)S(1)} async-done(((bf16[2,8,16,256]{3,1,0,2:T(8,128)(2,1)}), bf16[2,8,16,256]{3,1,0,2:T(8,128)(2,1)S(1)}, u32[]{:S(2)}, u32[]{:S(2)}) %all-to-all-start.4) | async-done | bytes 131104 | tf_op jit(solution)/shard_map/all_to_all | solution.py:282
  63.5 3.6 %all-to-all-start.2 = ((bf16[8,2,8,16,256]{4,3,2,1,0:T(8,128)(2,1)}), bf16[8,2,8,16,256]{4,3,2,1,0:T(8,128)(2,1)S(1)}, u32[]{:S(2)}, u32[]{:S(2)}) async-start(bf16[8,2,8,16,256]{4,3,2,1,0:T(8,128)(2,1)} %get-tuple-element.17), calls=%async_computation.2 | async-start | bytes 2097152 | tf_op jit(solution)/shard_map/all_to_all | solution.py:274
  67.2 0.2 fusion.1
  67.4 0.2 copy.35
  67.7 1.0 pad_maximum_fusion.1.pred_ref
  68.7 0.7 pad_maximum_fusion.grad_ref
  69.4 0.7 copy.34
  70.1 15.3 %shrink_0.1.refs_0_ = f32[2,32,256,512]{3,2,1,0:T(8,128)} custom-call(bf16[32,2048]{1,0:T(8,128)(2,1)} %bitcast.22, bf16[128,1024]{1,0:T(8,128)(2,1)} %pad_maximum_fusion.grad_ref, bf16[1024,128]{1,0:T(8,128)(2,1)} %pad_maximum_fusion.1.pred_ref), custom_call_target="tpu_custom_call" | custom-call | flops 7516192768 | bytes 8388608 | tf_op jit(solution)/shard_map/shrink_0/pallas_call | solution.py:202
  85.4 6.3 %all-to-all-done.2 = bf16[8,2,8,16,256]{4,3,2,1,0:T(8,128)(2,1)S(1)} async-done(((bf16[8,2,8,16,256]{4,3,2,1,0:T(8,128)(2,1)}), bf16[8,2,8,16,256]{4,3,2,1,0:T(8,128)(2,1)S(1)}, u32[]{:S(2)}, u32[]{:S(2)}) %all-to-all-start.2) | async-done | bytes 1048608 | tf_op jit(solution)/shard_map/all_to_all | solution.py:274
  91.9 6.8 %all_to_all.81 = bf16[2,8,16,256]{3,1,0,2:T(8,128)(2,1)S(1)} all-to-all(bf16[2,8,16,256]{3,1,0,2:T(8,128)(2,1)S(1)} %copy.37), channel_id=1, replica_groups=mesh['ap'=16,'pass'=2] {'pass'}, dimensions={2} | all-to-all | bytes 262144 | tf_op jit(solution)/shard_map/all_to_all | solution.py:282
  98.7 3.6 %all-to-all-start.1 = ((bf16[8,2,8,16,256]{4,3,2,1,0:T(8,128)(2,1)}), bf16[8,2,8,16,256]{4,3,2,1,0:T(8,128)(2,1)S(1)}, u32[]{:S(2)}, u32[]{:S(2)}) async-start(bf16[8,2,8,16,256]{4,3,2,1,0:T(8,128)(2,1)} %get-tuple-element.16), calls=%async_computation.1 | async-start | bytes 2097152 | tf_op jit(solution)/shard_map/all_to_all | solution.py:274
  102.3 0.7 copy.38
  103.0 15.3 %shrink_1.1.refs_0_ = f32[2,32,256,512]{3,2,1,0:T(8,128)} custom-call(bf16[32,2048]{1,0:T(8,128)(2,1)} %bitcast.20, bf16[128,1024]{1,0:T(8,128)(2,1)} %pad_maximum_fusion.grad_ref, bf16[1024,128]{1,0:T(8,128)(2,1)} %pad_maximum_fusion.1.pred_ref, f32[2,32,256,512]{3,2,1,0:T(8,128)} %shrink_0.1.refs_0_), custom_call_target="tpu_custom_call", output_to_operand_aliasing={{}: (3, {})} | custom-call | flops 7516192768 | bytes 8388608 | tf_op jit(solution)/shard_map/shrink_1/pallas_call | solution.py:202
  118.3 8.9 %all-to-all-done.1 = bf16[8,2,8,16,256]{4,3,2,1,0:T(8,128)(2,1)S(1)} async-done(((bf16[8,2,8,16,256]{4,3,2,1,0:T(8,128)(2,1)}), bf16[8,2,8,16,256]{4,3,2,1,0:T(8,128)(2,1)S(1)}, u32[]{:S(2)}, u32[]{:S(2)}) %all-to-all-start.1) | async-done | bytes 1048608 | tf_op jit(solution)/shard_map/all_to_all | solution.py:274
  127.4 6.8 %all_to_all.82 = bf16[2,8,16,256]{3,1,0,2:T(8,128)(2,1)S(1)} all-to-all(bf16[2,8,16,256]{3,1,0,2:T(8,128)(2,1)S(1)} %copy.39), channel_id=1, replica_groups=mesh['ap'=16,'pass'=2] {'pass'}, dimensions={2} | all-to-all | bytes 262144 | tf_op jit(solution)/shard_map/all_to_all | solution.py:282
  134.2 3.7 %all-to-all-start = ((bf16[8,2,8,16,256]{4,3,2,1,0:T(8,128)(2,1)}), bf16[8,2,8,16,256]{4,3,2,1,0:T(8,128)(2,1)S(1)}, u32[]{:S(2)}, u32[]{:S(2)}) async-start(bf16[8,2,8,16,256]{4,3,2,1,0:T(8,128)(2,1)} %get-tuple-element.15), calls=%async_computation | async-start | bytes 2097152 | tf_op jit(solution)/shard_map/all_to_all | solution.py:274
  138.0 0.7 copy.40
  138.6 15.3 %shrink_2.1.refs_0_ = f32[2,32,256,512]{3,2,1,0:T(8,128)} custom-call(bf16[32,2048]{1,0:T(8,128)(2,1)} %bitcast.21, bf16[128,1024]{1,0:T(8,128)(2,1)} %pad_maximum_fusion.grad_ref, bf16[1024,128]{1,0:T(8,128)(2,1)} %pad_maximum_fusion.1.pred_ref, f32[2,32,256,512]{3,2,1,0:T(8,128)} %shrink_1.1.refs_0_), custom_call_target="tpu_custom_call", output_to_operand_aliasing={{}: (3, {})} | custom-call | flops 7516192768 | bytes 8388608 | tf_op jit(solution)/shard_map/shrink_2/pallas_call | solution.py:202
  153.9 8.7 %all-to-all-done = bf16[8,2,8,16,256]{4,3,2,1,0:T(8,128)(2,1)S(1)} async-done(((bf16[8,2,8,16,256]{4,3,2,1,0:T(8,128)(2,1)}), bf16[8,2,8,16,256]{4,3,2,1,0:T(8,128)(2,1)S(1)}, u32[]{:S(2)}, u32[]{:S(2)}) %all-to-all-start) | async-done | bytes 1048608 | tf_op jit(solution)/shard_map/all_to_all | solution.py:274
  162.9 6.8 %all_to_all.83 = bf16[2,8,16,256]{3,1,0,2:T(8,128)(2,1)S(1)} all-to-all(bf16[2,8,16,256]{3,1,0,2:T(8,128)(2,1)S(1)} %copy.41), channel_id=1, replica_groups=mesh['ap'=16,'pass'=2] {'pass'}, dimensions={2} | all-to-all | bytes 262144 | tf_op jit(solution)/shard_map/all_to_all | solution.py:282
  169.7 0.7 copy.42
  170.4 15.3 %shrink_3.1 = f32[2,32,256,512]{3,2,1,0:T(8,128)} custom-call(bf16[32,2048]{1,0:T(8,128)(2,1)} %bitcast.19, bf16[128,1024]{1,0:T(8,128)(2,1)} %pad_maximum_fusion.grad_ref, bf16[1024,128]{1,0:T(8,128)(2,1)} %pad_maximum_fusion.1.pred_ref, f32[2,32,256,512]{3,2,1,0:T(8,128)} %shrink_2.1.refs_0_), custom_call_target="tpu_custom_call", output_to_operand_aliasing={{}: (3, {})} | custom-call | flops 7516192768 | bytes 8388608 | tf_op jit(solution)/shard_map/shrink_3/pallas_call | solution.py:202
  (15 shorter events, 0.8 us)
Async XLA Ops:
  7.7 3.7 %collective-permute-start.1 = (bf16[2,8,128,256]{3,2,1,0:T(8,128)(2,1)}, bf16[2,8,128,256]{3,2,1,0:T(8,128)(2,1)S(1)}, u32[]{:S(2)}, u32[]{:S(2)}) collective-permute-start(bf16[2,8,128,256]{3,2,1,0:T(8,128)(2,1)} %focus.1.refs_2_), channel_id=1, source_target_pairs={{0,2},{2,0},{4,6},{6,4},{8,10},{10,8},{12,14},{14,12},{16,18},{18,... | collective-permute-start | bytes 3145736 | tf_op jit(solution)/shard_map/ppermute | solution.py:247
  8.2 3.2 %collective-permute-start = (bf16[2,1024,128]{2,1,0:T(8,128)(2,1)}, bf16[2,1024,128]{2,1,0:T(8,128)(2,1)S(1)}, u32[]{:S(2)}, u32[]{:S(2)}) collective-permute-start(bf16[2,1024,128]{2,1,0:T(8,128)(2,1)} %refs_0_.1), channel_id=1, source_target_pairs={{0,2},{2,0},{4,6},{6,4},{8,10},{10,8},{12,14},{14,12},{16,18},{18,... | collective-permute-start | bytes 1572872 | tf_op jit(solution)/shard_map/ppermute | solution.py:245
  11.5 0.8 copy-start.1
  11.5 1.2 copy-start
  55.7 7.8 %all-to-all-start.4 = ((bf16[2,8,16,256]{3,1,0,2:T(8,128)(2,1)}), bf16[2,8,16,256]{3,1,0,2:T(8,128)(2,1)S(1)}, u32[]{:S(2)}, u32[]{:S(2)}) async-start(bf16[2,8,16,256]{3,1,0,2:T(8,128)(2,1)} %copy.33), calls=%async_computation.4 | async-start | bytes 262144 | tf_op jit(solution)/shard_map/all_to_all | solution.py:282
  63.5 28.1 %all-to-all-start.2 = ((bf16[8,2,8,16,256]{4,3,2,1,0:T(8,128)(2,1)}), bf16[8,2,8,16,256]{4,3,2,1,0:T(8,128)(2,1)S(1)}, u32[]{:S(2)}, u32[]{:S(2)}) async-start(bf16[8,2,8,16,256]{4,3,2,1,0:T(8,128)(2,1)} %get-tuple-element.17), calls=%async_computation.2 | async-start | bytes 2097152 | tf_op jit(solution)/shard_map/all_to_all | solution.py:274
  98.7 28.4 %all-to-all-start.1 = ((bf16[8,2,8,16,256]{4,3,2,1,0:T(8,128)(2,1)}), bf16[8,2,8,16,256]{4,3,2,1,0:T(8,128)(2,1)S(1)}, u32[]{:S(2)}, u32[]{:S(2)}) async-start(bf16[8,2,8,16,256]{4,3,2,1,0:T(8,128)(2,1)} %get-tuple-element.16), calls=%async_computation.1 | async-start | bytes 2097152 | tf_op jit(solution)/shard_map/all_to_all | solution.py:274
  134.2 28.4 %all-to-all-start = ((bf16[8,2,8,16,256]{4,3,2,1,0:T(8,128)(2,1)}), bf16[8,2,8,16,256]{4,3,2,1,0:T(8,128)(2,1)S(1)}, u32[]{:S(2)}, u32[]{:S(2)}) async-start(bf16[8,2,8,16,256]{4,3,2,1,0:T(8,128)(2,1)} %get-tuple-element.15), calls=%async_computation | async-start | bytes 2097152 | tf_op jit(solution)/shard_map/all_to_all | solution.py:274
